TPU v7x, 32 devices: a whole 2x2x4 slice. The times are simulated.
32 devices in a mesh: groups: 2 (over y), res: 8 (over z, x), seq: 2 (over core).
Axes of the slice: x: 2, y: 2, z: 4, core: 2. Of those that a mesh axis runs over, the one named last changes fastest.
Arguments:
- alignment: bfloat16 [128, 32, 256], P(('groups', 'seq'), 'res'), parts along dimension 0, may hold values from -6 to 6
- ln_gain: float32 [256], replicated, may hold values from 0.1 to 1.9
- proj_left: bfloat16 [256, 32], replicated, may hold values from -0.375 to 0.375
- proj_right: bfloat16 [256, 32], replicated, may hold values from -0.375 to 0.375
- out_weight: bfloat16 [1024, 128], replicated, may hold values from -4 to 4
- out_bias: float32 [128], replicated, may hold values from -3 to 3
Outputs:
- pair_update: bfloat16 [64, 32, 128], P(('groups', 'res'), 'seq'), parts along dimension 0
There are 2 independent parts, one for each index of `groups`. A program takes and returns all parts, laid end to end along the dimension named above; an argument that names none is the same for every part. Nothing has to cross between parts.
All inputs are finite; a program needn't handle non-finite values.
Results may differ from a plain program's by a relative error of at most 0.0095.
Values may be sent and summed in bfloat16 or wider, within the bound.
No kernel may reach another device: no remote copies, remote signals or barrier semaphores. Data moves between devices by JAX's collectives and lax.ppermute only.
A program may use at most 64 MiB of HBM per device.

v0:
```python
import math
import jax
import jax.numpy as jnp
from jax import lax
from jax.sharding import PartitionSpec as P


def normalize(alignment, ln_gain):
    values = alignment.astype(jnp.float32)
    centred = values - jnp.mean(values, axis=-1, keepdims=True)
    variance = jnp.mean(centred * centred, axis=-1, keepdims=True)
    return (centred * lax.rsqrt(variance + 1e-05) * ln_gain).astype(jnp.bfloat16)


def pair_block(left_flat, columns, weight_full, inv_count):
    channels = columns.shape[2]
    col_count = columns.shape[1]
    row_count = left_flat.shape[1] // channels
    block_width = math.gcd(col_count, 64)

    def advance(position, totals):
        column_block = lax.dynamic_slice_in_dim(columns, position * block_width, block_width, 1)
        right_flat = column_block.reshape(columns.shape[0], block_width * channels)
        outer_terms = (
            lax.dot_general(
                left_flat, right_flat, (((0,), (0,)), ((), ())), preferred_element_type=jnp.float32
            )
            * inv_count
        )
        outer_terms = outer_terms.reshape(row_count, channels, block_width, channels).transpose(
            0, 2, 1, 3
        )
        outer_terms = outer_terms.reshape(row_count * block_width, channels * channels)
        projected = jnp.dot(outer_terms, weight_full, precision=lax.Precision.HIGHEST)
        projected = projected.reshape(row_count, block_width, weight_full.shape[1])
        return lax.dynamic_update_slice_in_dim(totals, projected, position * block_width, 1)

    totals = jnp.zeros((row_count, col_count, weight_full.shape[1]), jnp.float32)
    return lax.fori_loop(0, col_count // block_width, advance, totals)


def on_device(alignment, ln_gain, proj_left, proj_right, out_weight, out_bias):
    seq_shards = lax.axis_size("seq")
    local_seqs = alignment.shape[0]
    local_res = alignment.shape[1]
    channels = proj_left.shape[1]
    inv_count = 1.0 / (local_seqs * seq_shards)
    normed = normalize(alignment, ln_gain)
    flat_rows = normed.reshape(-1, normed.shape[2])
    both_sides = jnp.dot(
        flat_rows, jnp.concatenate((proj_left, proj_right), 1), preferred_element_type=jnp.float32
    )
    both_sides = both_sides.astype(jnp.bfloat16).reshape(local_seqs, local_res, 2 * channels)
    left_side = both_sides[:, :, :channels]
    right_side = both_sides[:, :, channels:]
    weight_full = out_weight.astype(jnp.float32)
    left_all = lax.all_gather(left_side, "seq", axis=0, tiled=True)
    left_flat = left_all.reshape(left_all.shape[0], local_res * channels)
    right_all = lax.all_gather(right_side, "res", axis=1, tiled=True)
    split_right = right_all.reshape(
        local_seqs, seq_shards, right_all.shape[1] // seq_shards, channels
    )
    arrived = lax.all_to_all(split_right, "seq", split_axis=1, concat_axis=0, tiled=True)
    squeezed = arrived.reshape(arrived.shape[0], arrived.shape[2], arrived.shape[3])
    summed = pair_block(left_flat, squeezed, weight_full, inv_count)
    return (summed + out_bias).astype(jnp.bfloat16)


def solution(mesh):
    placed = (P(("groups", "seq"), "res", None), P(), P(), P(), P(), P())
    return jax.shard_map(
        on_device,
        mesh=mesh,
        in_specs=placed,
        out_specs=P(("groups", "res"), "seq", None),
        check_vma=False,
    )
```

profile of v0, /device:TPU:0, one launch (start us, length us, event | category | flops | bytes accessed | tf_op | source)
XLA Modules:
  0.0 44.9 jit_solution(8482532180802499849)
XLA Ops:
  0.0 0.0 copy-start
  0.0 0.0 copy-start.1
  0.0 1.0 %convert_reduce_fusion = f32[32,4]{1,0:T(8,128)S(1)} fusion(bf16[32,4,256]{2,1,0:T(4,128)(2,1)} %param.6), kind=kLoop, calls=%fused_computation.6 | loop fusion | flops 65408 | bytes 66048 | tf_op jit(solution)/shard_map/reduce_sum | solution.py:10
  1.0 0.0 copy-done.1
  1.1 0.2 fusion.4
  1.2 0.0 copy-start.4
  1.3 0.7 %copy-done.4 = f32[256]{0:T(256)S(1)} copy-done((f32[256]{0:T(256)S(1)}, f32[256]{0:T(256)}, u32[]{:S(2)}) %copy-start.4) | copy-done | bytes 1048
  1.9 0.1 fusion.6
  2.1 0.0 copy-start.2
  2.1 0.0 copy-start.3
  2.1 0.7 %copy-done.2 = bf16[256,32]{0,1:T(8,128)(2,1)S(1)} copy-done((bf16[256,32]{0,1:T(8,128)(2,1)S(1)}, bf16[256,32]{0,1:T(8,128)(2,1)}, u32[]{:S(2)}) %copy-start.2) | copy-done | bytes 16408
  2.8 0.0 copy-done.3
  2.8 0.1 convolution_convert_fusion
  2.9 0.1 copy.12
  3.1 0.1 fusion.11
  3.2 32.6 %all_gather.7 = bf16[32,32,32]{2,0,1:T(8,128)(2,1)S(1)} all-gather(bf16[32,4,32]{2,0,1:T(8,128)(2,1)S(1)} %copy.14), channel_id=1, replica_groups=mesh['groups'=2,'res'=8,'seq'=2] {'res'}, dimensions={1}, use_global_device_ids=true | all-gather | bytes 73728 | tf_op jit(solution)/shard_map/all_gather | solution.py:59
  35.7 0.1 copy.21
  35.9 0.9 %reshape.50 = bf16[2,2,8192]{2,1,0:T(2,128)(2,1)} reshape(bf16[2,32,16,32]{3,2,1,0:T(8,128)(2,1)S(1)} %bitcast.27) | data formatting | bytes 131072
  36.8 3.3 %all-to-all-start = ((bf16[2,2,8192]{2,1,0:T(2,128)(2,1)}), bf16[2,2,8192]{2,1,0:T(2,128)(2,1)S(1)}, u32[]{:S(2)}, u32[]{:S(2)}) async-start(bf16[2,2,8192]{2,1,0:T(2,128)(2,1)} %reshape.50), calls=%async_computation | async-start | bytes 131072 | tf_op jit(solution)/shard_map/all_to_all | solution.py:63
  40.1 2.0 %all_gather.6 = bf16[64,4,32]{2,1,0:T(4,128)(2,1)S(1)} all-gather(bf16[32,4,32]{2,1,0:T(4,128)(2,1)S(1)} %get-tuple-element.16), channel_id=1, replica_groups=mesh['groups'=2,'res'=8,'seq'=2] {'seq'}, dimensions={0}, use_global_device_ids=true | all-gather | bytes 24576 | tf_op jit(solution)/shard_map/all_gather | solution.py:57
  42.0 0.1 copy.13
  42.1 0.0 all-to-all-done
  42.2 0.2 reshape.51
  42.4 0.2 reshape.47
  42.6 0.2 convolution_multiply_fusion
  42.8 0.3 reshape.48
  43.1 0.3 copy.17
  43.4 0.0 copy-start.5
  43.4 0.5 %dot_general.15 = f32[4,16,1024]{2,1,0:T(8,128)S(1)} reshape(f32[4,16,32,32]{3,2,1,0:T(8,128)S(1)} %copy.17) | data formatting | bytes 524288 | tf_op jit(solution)/shard_map/while/body/eval_jaxpr/dot_general | solution.py:34
  43.9 0.0 copy-done
  43.9 0.1 copy-done.5
  44.0 0.9 %fusion = bf16[4,16,128]{2,1,0:T(8,128)(2,1)} fusion(f32[4,16,1024]{2,1,0:T(8,128)S(1)} %dot_general.15, bf16[1024,128]{1,0:T(8,128)(2,1)S(1)} %copy-done, f32[128]{0:T(128)S(1)} %copy-done.5), kind=kOutput, calls=%fused_computation.3 | convolution fusion | flops 100679680 | bytes 541184 | tf_op jit(solution)/shard_map/while/body/eval_jaxpr/dot_general | solution.py:34
  (5 shorter events, 0.1 us)
Async XLA Ops:
  0.0 43.9 %copy-start = (bf16[1024,128]{1,0:T(8,128)(2,1)S(1)}, bf16[1024,128]{1,0:T(8,128)(2,1)}, u32[]{:S(2)}) copy-start(bf16[1024,128]{1,0:T(8,128)(2,1)} %param.10) | copy-start | bytes 786436
  0.0 1.0 %copy-start.1 = (bf16[32,4,256]{2,1,0:T(4,128)(2,1)S(1)}, bf16[32,4,256]{2,1,0:T(4,128)(2,1)}, u32[]{:S(2)}) copy-start(bf16[32,4,256]{2,1,0:T(4,128)(2,1)} %param.6) | copy-start | bytes 196612
  1.2 0.7 %copy-start.4 = (f32[256]{0:T(256)S(1)}, f32[256]{0:T(256)}, u32[]{:S(2)}) copy-start(f32[256]{0:T(256)} %param.7) | copy-start | bytes 3076
  2.1 0.7 %copy-start.2 = (bf16[256,32]{0,1:T(8,128)(2,1)S(1)}, bf16[256,32]{0,1:T(8,128)(2,1)}, u32[]{:S(2)}) copy-start(bf16[256,32]{0,1:T(8,128)(2,1)} %param.9) | copy-start | bytes 49156
  2.1 0.7 %copy-start.3 = (bf16[256,32]{0,1:T(8,128)(2,1)S(1)}, bf16[256,32]{0,1:T(8,128)(2,1)}, u32[]{:S(2)}) copy-start(bf16[256,32]{0,1:T(8,128)(2,1)} %param.8) | copy-start | bytes 49156
  36.8 5.4 %all-to-all-start = ((bf16[2,2,8192]{2,1,0:T(2,128)(2,1)}), bf16[2,2,8192]{2,1,0:T(2,128)(2,1)S(1)}, u32[]{:S(2)}, u32[]{:S(2)}) async-start(bf16[2,2,8192]{2,1,0:T(2,128)(2,1)} %reshape.50), calls=%async_computation | async-start | bytes 131072 | tf_op jit(solution)/shard_map/all_to_all | solution.py:63
  43.4 0.7 %copy-start.5 = (f32[128]{0:T(128)S(1)}, f32[128]{0:T(128)}, u32[]{:S(2)}) copy-start(f32[128]{0:T(128)} %param.11) | copy-start | bytes 1540
where the time goes:
time: 45.3 us; the launch traced here: 44.9 us
  blocking collectives  34.5 us (76%)
  local copies, waits for them, and re-layouts  4.41 us (10%)
  starting transfers between devices  3.29 us (7%)
  other arithmetic  1.34 us (3%)
  matrix products  1.15 us (3%)
    all_gather x1, blocking collectives, on_device(): right_all = lax.all_gather(right_side, 'res', axis=1, tiled=True)  32.6 us
    all_to_all x1, starting transfers between devices, on_device(): lax.all_to_all(split_right, 'seq', split_axis=1, concat_axis=0, tiled=True)  3.29 us
    unnamed x14, local copies, waits for them, and re-layouts  2.61 us
    all_gather x1, blocking collectives, on_device(): left_all = lax.all_gather(left_side, 'seq', axis=0, tiled=True)  1.98 us
    reduce_sum x1, other arithmetic, normalize(): centred = values - jnp.mean(values, axis=-1, keepdims=True)  1.02 us
  transfers between devices with their start and end apart: 1, of which 0 were waited for; matrix products, arithmetic and copies ran while one was open for 0% of the time, Pallas kernels for 0%

commit v1 on v0

--- a/solution.py
+++ b/solution.py
@@ -56,7 +56,12 @@
     weight_full = out_weight.astype(jnp.float32)
     left_all = lax.all_gather(left_side, "seq", axis=0, tiled=True)
     left_flat = left_all.reshape(left_all.shape[0], local_res * channels)
-    right_all = lax.all_gather(right_side, "res", axis=1, tiled=True)
+    ring = [right_side]
+    for hop in range(7):
+        ring.append(lax.ppermute(ring[-1], "res", [(dev, (dev + 1) % 8) for dev in range(8)]))
+    right_all = jnp.roll(
+        jnp.concatenate(ring[::-1], axis=1), (lax.axis_index("res") + 1) * ring[0].shape[1], axis=1
+    )
     split_right = right_all.reshape(
         local_seqs, seq_shards, right_all.shape[1] // seq_shards, channels
     )

time: 45.3 us -> 59.1 us (1.30)
  waiting for transfers between devices: 0.01 us -> 43 us
  blocking collectives: 34.5 us -> 5.63 us
    ppermute x0 -> x7, waiting for transfers between devices: none -> 43 us  [on_device(): lax.ppermute(ring[-1], 'res', [(dev, (dev + 1) % 8) for dev in range(8)])]
    all_gather x1 -> x0, blocking collectives: 32.6 us -> none  [on_device(): right_all = lax.all_gather(right_side, 'res', axis=1, tiled=True)]
    all_to_all x0 -> x1, blocking collectives: none -> 3.79 us  [on_device(): lax.all_to_all(split_right, 'seq', split_axis=1, concat_axis=0, tiled=True)]
    all_to_all x1 -> x0, starting transfers between devices: 3.29 us -> none  [on_device(): lax.all_to_all(split_right, 'seq', split_axis=1, concat_axis=0, tiled=True)]
    ppermute x0 -> x7, starting transfers between devices: none -> 3.04 us  [on_device(): lax.ppermute(ring[-1], 'res', [(dev, (dev + 1) % 8) for dev in range(8)])]
    unnamed x14, local copies, waits for them, and re-layouts: 2.61 us -> 1.99 us
  transfers between devices with their start and end apart: 1 -> 7, of which waited for: 0 -> 7; matrix products, arithmetic and copies ran while one was open for 0% -> 0% of each run, Pallas kernels for 0% -> 0%
where the time goes in v1:
time: 59.1 us; the launch traced here: 58.7 us
  waiting for transfers between devices  43 us (73%)
  blocking collectives  5.63 us (10%)
  local copies, waits for them, and re-layouts  4.36 us (7%)
  starting transfers between devices  3.04 us (5%)
  other arithmetic  1.34 us (2%)
  matrix products  1.16 us (2%)
    ppermute x7, waiting for transfers between devices, on_device(): lax.ppermute(ring[-1], 'res', [(dev, (dev + 1) % 8) for dev in range(8)])  43 us
    all_to_all x1, blocking collectives, on_device(): lax.all_to_all(split_right, 'seq', split_axis=1, concat_axis=0, tiled=True)  3.79 us
    ppermute x7, starting transfers between devices, on_device(): lax.ppermute(ring[-1], 'res', [(dev, (dev + 1) % 8) for dev in range(8)])  3.04 us
    unnamed x14, local copies, waits for them, and re-layouts  1.99 us
    all_gather x1, blocking collectives, on_device(): left_all = lax.all_gather(left_side, 'seq', axis=0, tiled=True)  1.84 us
  transfers between devices with their start and end apart: 7, of which 7 were waited for; matrix products, arithmetic and copies ran while one was open for 0% of the time, Pallas kernels for 0%

profile of v1, /device:TPU:0, one launch (start us, length us, event | category | flops | bytes accessed | tf_op | source)
XLA Modules:
  0.0 58.7 jit_solution(11480057375661233241)
XLA Ops:
  0.0 0.0 copy-start
  0.0 0.0 copy-start.1
  0.0 1.0 %convert_reduce_fusion = f32[32,4]{1,0:T(8,128)S(1)} fusion(bf16[32,4,256]{2,1,0:T(4,128)(2,1)} %param.6), kind=kLoop, calls=%fused_computation.6 | loop fusion | flops 65408 | bytes 66048 | tf_op jit(solution)/shard_map/reduce_sum | solution.py:10
  1.0 0.0 copy-done.1
  1.1 0.2 fusion.4
  1.2 0.0 copy-start.4
  1.3 0.7 %copy-done.4 = f32[256]{0:T(256)S(1)} copy-done((f32[256]{0:T(256)S(1)}, f32[256]{0:T(256)}, u32[]{:S(2)}) %copy-start.4) | copy-done | bytes 1048
  1.9 0.1 fusion.6
  2.1 0.0 copy-start.2
  2.1 0.0 copy-start.3
  2.1 0.7 %copy-done.2 = bf16[256,32]{0,1:T(8,128)(2,1)S(1)} copy-done((bf16[256,32]{0,1:T(8,128)(2,1)S(1)}, bf16[256,32]{0,1:T(8,128)(2,1)}, u32[]{:S(2)}) %copy-start.2) | copy-done | bytes 16408
  2.8 0.0 copy-done.3
  2.8 0.1 convolution_convert_fusion
  2.9 0.1 copy.12
  3.1 0.1 fusion.11
  3.2 3.0 %collective-permute-start = (bf16[32,4,32]{2,1,0:T(4,128)(2,1)S(1)}, bf16[32,4,32]{2,1,0:T(4,128)(2,1)S(1)}, u32[]{:S(2)}, u32[]{:S(2)}) collective-permute-start(bf16[32,4,32]{2,1,0:T(4,128)(2,1)S(1)} %get-tuple-element.15), channel_id=1, source_target_pairs={{0,2},{2,4},{4,6},{6,8},{8,10},{10,12},{12,14},{14,0},{1,3},{3,5},... | collective-permute-start | bytes 24584 | tf_op jit(solution)/shard_map/ppermute | solution.py:61
  6.2 4.9 %collective-permute-done = bf16[32,4,32]{2,1,0:T(4,128)(2,1)S(1)} collective-permute-done((bf16[32,4,32]{2,1,0:T(4,128)(2,1)S(1)}, bf16[32,4,32]{2,1,0:T(4,128)(2,1)S(1)}, u32[]{:S(2)}, u32[]{:S(2)}) %collective-permute-start) | collective-permute-done | bytes 8224 | tf_op jit(solution)/shard_map/ppermute | solution.py:61
  11.1 0.0 collective-permute-start.1
  11.1 6.6 %collective-permute-done.1 = bf16[32,4,32]{2,1,0:T(4,128)(2,1)S(1)} collective-permute-done((bf16[32,4,32]{2,1,0:T(4,128)(2,1)S(1)}, bf16[32,4,32]{2,1,0:T(4,128)(2,1)S(1)}, u32[]{:S(2)}, u32[]{:S(2)}) %collective-permute-start.1) | collective-permute-done | bytes 8224 | tf_op jit(solution)/shard_map/ppermute | solution.py:61
  17.7 0.0 collective-permute-start.2
  17.7 6.6 %collective-permute-done.2 = bf16[32,4,32]{2,1,0:T(4,128)(2,1)S(1)} collective-permute-done((bf16[32,4,32]{2,1,0:T(4,128)(2,1)S(1)}, bf16[32,4,32]{2,1,0:T(4,128)(2,1)S(1)}, u32[]{:S(2)}, u32[]{:S(2)}) %collective-permute-start.2) | collective-permute-done | bytes 8224 | tf_op jit(solution)/shard_map/ppermute | solution.py:61
  24.3 0.0 collective-permute-start.3
  24.4 6.6 %collective-permute-done.3 = bf16[32,4,32]{2,1,0:T(4,128)(2,1)S(1)} collective-permute-done((bf16[32,4,32]{2,1,0:T(4,128)(2,1)S(1)}, bf16[32,4,32]{2,1,0:T(4,128)(2,1)S(1)}, u32[]{:S(2)}, u32[]{:S(2)}) %collective-permute-start.3) | collective-permute-done | bytes 8224 | tf_op jit(solution)/shard_map/ppermute | solution.py:61
  31.0 0.0 collective-permute-start.4
  31.0 6.9 %collective-permute-done.4 = bf16[32,4,32]{2,1,0:T(4,128)(2,1)S(1)} collective-permute-done((bf16[32,4,32]{2,1,0:T(4,128)(2,1)S(1)}, bf16[32,4,32]{2,1,0:T(4,128)(2,1)S(1)}, u32[]{:S(2)}, u32[]{:S(2)}) %collective-permute-start.4) | collective-permute-done | bytes 8224 | tf_op jit(solution)/shard_map/ppermute | solution.py:61
  37.9 0.0 collective-permute-start.5
  37.9 6.6 %collective-permute-done.5 = bf16[32,4,32]{2,1,0:T(4,128)(2,1)S(1)} collective-permute-done((bf16[32,4,32]{2,1,0:T(4,128)(2,1)S(1)}, bf16[32,4,32]{2,1,0:T(4,128)(2,1)S(1)}, u32[]{:S(2)}, u32[]{:S(2)}) %collective-permute-start.5) | collective-permute-done | bytes 8224 | tf_op jit(solution)/shard_map/ppermute | solution.py:61
  44.5 0.0 collective-permute-start.6
  44.5 1.8 %all_gather.3 = bf16[64,4,32]{2,1,0:T(4,128)(2,1)S(1)} all-gather(bf16[32,4,32]{2,1,0:T(4,128)(2,1)S(1)} %get-tuple-element.16), channel_id=1, replica_groups=mesh['groups'=2,'res'=8,'seq'=2] {'seq'}, dimensions={0}, use_global_device_ids=true | all-gather | bytes 24576 | tf_op jit(solution)/shard_map/all_gather | solution.py:57
  46.4 0.1 copy.13
  46.5 4.7 %collective-permute-done.6 = bf16[32,4,32]{2,1,0:T(4,128)(2,1)S(1)} collective-permute-done((bf16[32,4,32]{2,1,0:T(4,128)(2,1)S(1)}, bf16[32,4,32]{2,1,0:T(4,128)(2,1)S(1)}, u32[]{:S(2)}, u32[]{:S(2)}) %collective-permute-start.6) | collective-permute-done | bytes 8224 | tf_op jit(solution)/shard_map/ppermute | solution.py:61
  51.1 0.5 concatenate.10
  51.7 0.1 constant_dynamic-slice_fusion
  51.8 0.3 reshape.50
  52.1 3.8 %all_to_all.15 = bf16[2,2,8192]{2,1,0:T(2,128)(2,1)S(1)} all-to-all(bf16[2,2,8192]{2,1,0:T(2,128)(2,1)S(1)} %reshape.50), channel_id=1, replica_groups=mesh['groups'=2,'res'=8,'seq'=2] {'seq'}, dimensions={0} | all-to-all | bytes 131072 | tf_op jit(solution)/shard_map/all_to_all | solution.py:68
  55.9 0.2 reshape.51
  56.1 0.2 reshape.47
  56.4 0.2 convolution_multiply_fusion
  56.5 0.3 reshape.48
  56.8 0.3 copy.15
  57.1 0.0 copy-start.5
  57.2 0.5 dot_general.15
  57.6 0.0 copy-done
  57.6 0.1 copy-done.5
  57.8 0.9 %fusion = bf16[4,16,128]{2,1,0:T(8,128)(2,1)} fusion(f32[4,16,1024]{2,1,0:T(8,128)S(1)} %dot_general.15, bf16[1024,128]{1,0:T(8,128)(2,1)S(1)} %copy-done, f32[128]{0:T(128)S(1)} %copy-done.5), kind=kOutput, calls=%fused_computation.3 | convolution fusion | flops 100679680 | bytes 541184 | tf_op jit(solution)/shard_map/while/body/eval_jaxpr/dot_general | solution.py:34
  (5 shorter events, 0.1 us)
Async XLA Ops:
  0.0 57.6 %copy-start = (bf16[1024,128]{1,0:T(8,128)(2,1)S(1)}, bf16[1024,128]{1,0:T(8,128)(2,1)}, u32[]{:S(2)}) copy-start(bf16[1024,128]{1,0:T(8,128)(2,1)} %param.10) | copy-start | bytes 786436
  0.0 1.0 %copy-start.1 = (bf16[32,4,256]{2,1,0:T(4,128)(2,1)S(1)}, bf16[32,4,256]{2,1,0:T(4,128)(2,1)}, u32[]{:S(2)}) copy-start(bf16[32,4,256]{2,1,0:T(4,128)(2,1)} %param.6) | copy-start | bytes 196612
  1.2 0.7 %copy-start.4 = (f32[256]{0:T(256)S(1)}, f32[256]{0:T(256)}, u32[]{:S(2)}) copy-start(f32[256]{0:T(256)} %param.7) | copy-start | bytes 3076
  2.1 0.7 %copy-start.2 = (bf16[256,32]{0,1:T(8,128)(2,1)S(1)}, bf16[256,32]{0,1:T(8,128)(2,1)}, u32[]{:S(2)}) copy-start(bf16[256,32]{0,1:T(8,128)(2,1)} %param.9) | copy-start | bytes 49156
  2.1 0.7 %copy-start.3 = (bf16[256,32]{0,1:T(8,128)(2,1)S(1)}, bf16[256,32]{0,1:T(8,128)(2,1)}, u32[]{:S(2)}) copy-start(bf16[256,32]{0,1:T(8,128)(2,1)} %param.8) | copy-start | bytes 49156
  3.2 8.0 %collective-permute-start = (bf16[32,4,32]{2,1,0:T(4,128)(2,1)S(1)}, bf16[32,4,32]{2,1,0:T(4,128)(2,1)S(1)}, u32[]{:S(2)}, u32[]{:S(2)}) collective-permute-start(bf16[32,4,32]{2,1,0:T(4,128)(2,1)S(1)} %get-tuple-element.15), channel_id=1, source_target_pairs={{0,2},{2,4},{4,6},{6,8},{8,10},{10,12},{12,14},{14,0},{1,3},{3,5},... | collective-permute-start | bytes 24584 | tf_op jit(solution)/shard_map/ppermute | solution.py:61
  11.1 6.6 %collective-permute-start.1 = (bf16[32,4,32]{2,1,0:T(4,128)(2,1)S(1)}, bf16[32,4,32]{2,1,0:T(4,128)(2,1)S(1)}, u32[]{:S(2)}, u32[]{:S(2)}) collective-permute-start(bf16[32,4,32]{2,1,0:T(4,128)(2,1)S(1)} %collective-permute-done), channel_id=1, source_target_pairs={{0,2},{2,4},{4,6},{6,8},{8,10},{10,12},{12,14},{14,0},{1,3},{3,5},... | collective-permute-start | bytes 24584 | tf_op jit(solution)/shard_map/ppermute | solution.py:61
  17.7 6.6 %collective-permute-start.2 = (bf16[32,4,32]{2,1,0:T(4,128)(2,1)S(1)}, bf16[32,4,32]{2,1,0:T(4,128)(2,1)S(1)}, u32[]{:S(2)}, u32[]{:S(2)}) collective-permute-start(bf16[32,4,32]{2,1,0:T(4,128)(2,1)S(1)} %collective-permute-done.1), channel_id=1, source_target_pairs={{0,2},{2,4},{4,6},{6,8},{8,10},{10,12},{12,14},{14,0},{1,3},{3,5},... | collective-permute-start | bytes 24584 | tf_op jit(solution)/shard_map/ppermute | solution.py:61
  24.3 6.6 %collective-permute-start.3 = (bf16[32,4,32]{2,1,0:T(4,128)(2,1)S(1)}, bf16[32,4,32]{2,1,0:T(4,128)(2,1)S(1)}, u32[]{:S(2)}, u32[]{:S(2)}) collective-permute-start(bf16[32,4,32]{2,1,0:T(4,128)(2,1)S(1)} %collective-permute-done.2), channel_id=1, source_target_pairs={{0,2},{2,4},{4,6},{6,8},{8,10},{10,12},{12,14},{14,0},{1,3},{3,5},... | collective-permute-start | bytes 24584 | tf_op jit(solution)/shard_map/ppermute | solution.py:61
  31.0 7.0 %collective-permute-start.4 = (bf16[32,4,32]{2,1,0:T(4,128)(2,1)S(1)}, bf16[32,4,32]{2,1,0:T(4,128)(2,1)S(1)}, u32[]{:S(2)}, u32[]{:S(2)}) collective-permute-start(bf16[32,4,32]{2,1,0:T(4,128)(2,1)S(1)} %collective-permute-done.3), channel_id=1, source_target_pairs={{0,2},{2,4},{4,6},{6,8},{8,10},{10,12},{12,14},{14,0},{1,3},{3,5},... | collective-permute-start | bytes 24584 | tf_op jit(solution)/shard_map/ppermute | solution.py:61
  37.9 6.6 %collective-permute-start.5 = (bf16[32,4,32]{2,1,0:T(4,128)(2,1)S(1)}, bf16[32,4,32]{2,1,0:T(4,128)(2,1)S(1)}, u32[]{:S(2)}, u32[]{:S(2)}) collective-permute-start(bf16[32,4,32]{2,1,0:T(4,128)(2,1)S(1)} %collective-permute-done.4), channel_id=1, source_target_pairs={{0,2},{2,4},{4,6},{6,8},{8,10},{10,12},{12,14},{14,0},{1,3},{3,5},... | collective-permute-start | bytes 24584 | tf_op jit(solution)/shard_map/ppermute | solution.py:61
  44.5 6.6 %collective-permute-start.6 = (bf16[32,4,32]{2,1,0:T(4,128)(2,1)S(1)}, bf16[32,4,32]{2,1,0:T(4,128)(2,1)S(1)}, u32[]{:S(2)}, u32[]{:S(2)}) collective-permute-start(bf16[32,4,32]{2,1,0:T(4,128)(2,1)S(1)} %collective-permute-done.5), channel_id=1, source_target_pairs={{0,2},{2,4},{4,6},{6,8},{8,10},{10,12},{12,14},{14,0},{1,3},{3,5},... | collective-permute-start | bytes 24584 | tf_op jit(solution)/shard_map/ppermute | solution.py:61
  57.1 0.7 %copy-start.5 = (f32[128]{0:T(128)S(1)}, f32[128]{0:T(128)}, u32[]{:S(2)}) copy-start(f32[128]{0:T(128)} %param.11) | copy-start | bytes 1540
